TPU v7x, 32 devices: a 4x2x2 block of a 4x4x8 slice. The times are simulated.
32 devices in a mesh: dp: 4 (over y, z), tp: 8 (over x, core).
Axes of the slice: x: 4, y: 2, z: 2, core: 2. Of those that a mesh axis runs over, the one named last changes fastest.
The devices are a block of a 4x4x8 slice.
Arguments:
- x_tokens: bfloat16 [4, 2048, 2048], P('dp', 'tp'), parts along dimension 0
- ln1_gain: float32 [2, 2048], replicated
- ln1_bias: float32 [2, 2048], replicated
- ln2_gain: float32 [2, 2048], replicated
- ln2_bias: float32 [2, 2048], replicated
- w_qkv: bfloat16 [2, 2048, 3, 16, 128], P(None, None, None, 'tp')
- w_out: bfloat16 [2, 16, 128, 2048], P(None, 'tp')
- b_out: float32 [2, 2048], replicated
- w_up: bfloat16 [2, 2048, 8192], P(None, None, 'tp')
- b_up: float32 [2, 8192], P(None, 'tp')
- w_down: bfloat16 [2, 8192, 2048], P(None, 'tp')
- b_down: float32 [2, 2048], replicated
Outputs:
- output: bfloat16 [4, 2048, 2048], P('dp', 'tp'), parts along dimension 0
There are 4 independent parts. A program takes and returns all parts, laid end to end along the dimension named above; an argument that names none is the same for every part.
All inputs are finite; a program needn't handle non-finite values.
Results may differ from a plain program's by a relative error of at most 0.0104569.
Values are sent between devices in bfloat16 or wider.
A program may use at most 768 MiB of HBM per device.

v0:
```python
import math
import jax
import jax.numpy as jnp
from jax import lax
from jax.sharding import PartitionSpec as P


def layer_norm(resid, gain, shift):
    row_mean = jnp.mean(resid, axis=-1, keepdims=True)
    centered = resid - row_mean
    variance = jnp.mean(centered * centered, axis=-1, keepdims=True)
    return (centered * lax.rsqrt(variance + 1e-5) * gain + shift).astype(jnp.bfloat16)


def solution(mesh):
    tp_size = mesh.shape["tp"]

    def scatter_rows(partial):
        batch, seq_len, width = partial.shape
        pieces = partial.astype(jnp.bfloat16).reshape(batch, tp_size, seq_len // tp_size, width)
        received = lax.all_to_all(pieces, "tp", 1, 1, tiled=True)
        return jnp.sum(received.astype(jnp.float32), axis=1)

    def local_forward(x_local, ln1_gain, ln1_bias, ln2_gain, ln2_bias, w_qkv, w_out, b_out, w_up, b_up, w_down, b_down):
        seq_len = x_local.shape[1] * tp_size
        scale = 1.0 / math.sqrt(w_out.shape[2])
        positions = jnp.arange(seq_len)
        causal = positions[:, None] >= positions[None, :]
        resid = x_local.astype(jnp.float32)
        for layer in range(w_qkv.shape[0]):
            normed = layer_norm(resid, ln1_gain[layer], ln1_bias[layer])
            gathered = lax.all_gather(normed, "tp", axis=1, tiled=True)
            qkv_proj = jnp.einsum("bsd,dthe->tbhse", gathered, w_qkv[layer], preferred_element_type=jnp.float32).astype(jnp.bfloat16)
            scores = jnp.einsum("bhqe,bhke->bhqk", qkv_proj[0], qkv_proj[1], preferred_element_type=jnp.float32) * scale
            attn_probs = jax.nn.softmax(jnp.where(causal, scores, -1e30), axis=-1).astype(jnp.bfloat16)
            attn_heads = jnp.einsum("bhqk,bhke->bhqe", attn_probs, qkv_proj[2], preferred_element_type=jnp.float32).astype(jnp.bfloat16)
            partial = jnp.einsum("cirf,ife->cre", attn_heads, w_out[layer], preferred_element_type=jnp.float32)
            resid = resid + (scatter_rows(partial) + b_out[layer])
            normed_mlp = layer_norm(resid, ln2_gain[layer], ln2_bias[layer])
            gathered_mlp = lax.all_gather(normed_mlp, "tp", axis=1, tiled=True)
            pre_act = jnp.einsum("bsd,df->bsf", gathered_mlp, w_up[layer], preferred_element_type=jnp.float32) + b_up[layer]
            hidden = jax.nn.gelu(pre_act, approximate=True).astype(jnp.bfloat16)
            partial_mlp = jnp.einsum("bsf,fd->bsd", hidden, w_down[layer], preferred_element_type=jnp.float32)
            resid = resid + (scatter_rows(partial_mlp) + b_down[layer])
        return resid.astype(jnp.bfloat16)

    rows_spec = P("dp", "tp", None)
    in_specs = (rows_spec, P(), P(), P(), P(), P(None, None, None, "tp", None), P(None, "tp", None, None), P(), P(None, None, "tp"), P(None, "tp"), P(None, "tp", None), P())
    return jax.shard_map(local_forward, mesh=mesh, in_specs=in_specs, out_specs=rows_spec, check_vma=False)
```

profile of v0, /device:TPU:81, one launch (start us, length us, event | category | flops | bytes accessed | tf_op | source)
XLA Modules:
  0.0 773.5 jit_solution(18355282130795484642)
XLA Ops:
  6.5 0.0 all-gather.5.cloned.1.call-start
  6.6 0.8 fusion.123
  7.4 0.8 fusion.124
  8.2 1.4 convert_reduce_fusion.4
  9.6 1.6 fusion.88
  11.3 2.7 fusion.91
  13.9 0.1 all-gather.5.cloned.1.call-update
  14.0 4.2 iota_compare_fusion
  18.2 8.3 %fusion.119 = (bf16[1,2048,3,2,128]{4,3,2,1,0:T(2,128)(2,1)}, bf16[1,2048,3,2,128]{4,3,2,1,0:T(2,128)(2,1)S(1)}) fusion(bf16[2,2048,3,2,128]{4,3,2,1,0:T(2,128)(2,1)} %param.17), kind=kLoop, calls=%fused_computation.139 | loop fusion | bytes 12582912 | tf_op jit(solution)/shard_map/slice | solution.py:33
  26.5 38.6 %all-gather.5.cloned.1.call-done = bf16[1,2048,2048]{2,1,0:T(8,128)(2,1)} async-done(((bf16[1,256,2048]{2,1,0:T(8,128)(2,1)}), bf16[1,2048,2048]{2,1,0:T(8,128)(2,1)}) %all-gather.5.cloned.1.call-update) | async-done | bytes 8388624 | tf_op jit(solution)/shard_map/all_gather | solution.py:32
  65.1 10.2 %fusion.81 = bf16[3,1,2,2048,128]{4,3,2,0,1:T(8,128)(2,1)} fusion(bf16[1,2048,3,2,128]{4,3,2,1,0:T(2,128)(2,1)S(1)} %get-tuple-element.10, bf16[1,2048,2048]{2,1,0:T(8,128)(2,1)} %all-gather.5.cloned.1.call-done), kind=kOutput, calls=%fused_computation.81 | convolution fusion | flops 6444023808 | bytes 14680064 | tf_op jit(solution)/shard_map/bsd,dthe->tbhse/dot_general | solution.py:33
  75.3 19.0 %fusion.127 = (f32[2,2048]{1,0:T(2,128)S(1)}, f32[2,2048,2048]{1,2,0:T(8,128)}) fusion(pred[2048,2048]{0,1:T(8,128)(4,1)} %iota_compare_fusion, bf16[3,1,2,2048,128]{4,3,2,0,1:T(8,128)(2,1)} %fusion.81), kind=kOutput, calls=%fused_computation.147 | convolution fusion | flops 2181040128 | bytes 39862272 | tf_op jit(solution)/shard_map/sub | solution.py:35
  94.3 0.0 copy-start.4
  94.3 14.4 %fusion.85 = bf16[2,2048,128]{2,1,0:T(8,128)(2,1)S(1)} fusion(f32[2,2048,2048]{1,2,0:T(8,128)} %get-tuple-element.26, f32[2,2048]{1,0:T(2,128)S(1)} %get-tuple-element.25, bf16[3,1,2,2048,128]{4,3,2,0,1:T(8,128)(2,1)} %fusion.81), kind=kOutput, calls=%fused_computation.83 | convolution fusion | flops 2164785152 | bytes 35667968 | tf_op jit(solution)/shard_map/bhqk,bhke->bhqe/dot_general | solution.py:36
  108.7 0.0 copy-done.4
  108.7 4.6 bitcast_convert_fusion.1
  113.3 5.3 all-to-all-start
  118.6 0.2 all-gather.7.cloned.1.call-start
  118.8 0.0 copy-done.6
  118.8 0.0 copy-done.7
  118.8 0.0 copy-done.8
  118.8 0.0 copy-start
  118.9 93.3 %all-to-all-done = bf16[1,8,256,2048]{3,2,0,1:T(8,128)(2,1)} async-done(((bf16[1,8,256,2048]{3,2,0,1:T(8,128)(2,1)}), bf16[1,8,256,2048]{3,2,0,1:T(8,128)(2,1)}, u32[]{:S(2)}, u32[]{:S(2)}) %all-to-all-start) | async-done | bytes 8388640 | tf_op jit(solution)/shard_map/all_to_all | solution.py:21
  212.2 5.3 convert_reduce_fusion.3
  217.5 0.0 copy-done
  217.5 0.4 fusion.114
  217.9 0.0 copy-start.10
  217.9 0.5 multiply_reduce_fusion.2
  218.4 1.6 add_convert_fusion.2
  219.9 0.1 all-gather.7.cloned.1.call-update
  220.0 0.0 copy-done.10
  220.0 46.7 %all-gather.7.cloned.1.call-done = bf16[1,2048,2048]{2,1,0:T(8,128)(2,1)} async-done(((bf16[1,256,2048]{2,1,0:T(8,128)(2,1)}), bf16[1,2048,2048]{2,1,0:T(8,128)(2,1)}) %all-gather.7.cloned.1.call-update) | async-done | bytes 8388624 | tf_op jit(solution)/shard_map/all_gather | solution.py:40
  266.7 25.3 %convolution_convert_fusion.1 = bf16[2048,2048]{1,0:T(8,128)(2,1)} fusion(bf16[1,2048,2048]{2,1,0:T(8,128)(2,1)} %all-gather.7.cloned.1.call-done, bf16[2,1024,2048]{2,1,0:T(8,128)(2,1)} %param.22, f32[1024]{0:T(1024)S(1)} %bitcast.209, bf16[2,2048,1024]{2,1,0:T(8,128)(2,1)} %param.20), kind=kOutput, calls=%fused_computation.52 | convolution fusion | flops 17205035008 | bytes 25169920 | tf_op jit(solution)/shard_map/bsf,fd->bsd/dot_general | solution.py:43
  292.1 5.3 all-to-all-start.1
  297.4 0.4 all-gather.9.cloned.1.call-start
  297.8 0.0 copy-done.9
  297.8 93.2 %all-to-all-done.1 = bf16[1,8,256,2048]{3,2,0,1:T(8,128)(2,1)} async-done(((bf16[1,8,256,2048]{3,2,0,1:T(8,128)(2,1)}), bf16[1,8,256,2048]{3,2,0,1:T(8,128)(2,1)}, u32[]{:S(2)}, u32[]{:S(2)}) %all-to-all-start.1) | async-done | bytes 8388640 | tf_op jit(solution)/shard_map/all_to_all | solution.py:21
  391.0 5.4 convert_reduce_fusion.2
  396.4 0.7 fusion.117
  397.1 0.0 copy-start.3
  397.2 0.3 multiply_reduce_fusion.1
  397.5 1.0 copy-done.1
  398.5 1.4 add_convert_fusion.1
  399.9 0.1 all-gather.9.cloned.1.call-update
  400.0 0.1 all-gather.11.cloned.1.call-start
  400.1 46.6 %all-gather.9.cloned.1.call-done = bf16[1,2048,2048]{2,1,0:T(8,128)(2,1)} async-done(((bf16[1,256,2048]{2,1,0:T(8,128)(2,1)}), bf16[1,2048,2048]{2,1,0:T(8,128)(2,1)}) %all-gather.9.cloned.1.call-update) | async-done | bytes 8388624 | tf_op jit(solution)/shard_map/all_gather | solution.py:32
  446.7 0.0 copy-done.3
  446.7 10.2 %fusion.78 = bf16[3,1,2,2048,128]{4,3,2,0,1:T(8,128)(2,1)} fusion(bf16[1,2048,3,2,128]{4,3,2,1,0:T(2,128)(2,1)S(1)} %copy-done.3, bf16[1,2048,2048]{2,1,0:T(8,128)(2,1)} %all-gather.9.cloned.1.call-done), kind=kOutput, calls=%fused_computation.80 | convolution fusion | flops 6444023808 | bytes 14680064 | tf_op jit(solution)/shard_map/bsd,dthe->tbhse/dot_general | solution.py:33
  456.9 19.0 %fusion.128 = (f32[2,2048]{1,0:T(2,128)S(1)}, f32[2,2048,2048]{1,2,0:T(8,128)}) fusion(pred[2048,2048]{0,1:T(8,128)(4,1)} %iota_compare_fusion, bf16[3,1,2,2048,128]{4,3,2,0,1:T(8,128)(2,1)} %fusion.78), kind=kOutput, calls=%fused_computation.148 | convolution fusion | flops 2181040128 | bytes 39862272 | tf_op jit(solution)/shard_map/sub | solution.py:35
  475.9 0.0 copy-start.5
  475.9 14.4 %fusion.84 = bf16[2,2048,128]{2,1,0:T(8,128)(2,1)S(1)} fusion(f32[2,2048,2048]{1,2,0:T(8,128)} %get-tuple-element.28, f32[2,2048]{1,0:T(2,128)S(1)} %get-tuple-element.27, bf16[3,1,2,2048,128]{4,3,2,0,1:T(8,128)(2,1)} %fusion.78), kind=kOutput, calls=%fused_computation.82 | convolution fusion | flops 2164785152 | bytes 35667968 | tf_op jit(solution)/shard_map/bhqk,bhke->bhqe/dot_general | solution.py:36
  490.3 0.0 copy-done.5
  490.3 2.6 bitcast_convert_fusion
  492.8 97.2 %all_to_all.20 = bf16[1,8,256,2048]{3,2,0,1:T(8,128)(2,1)S(1)} all-to-all(bf16[1,8,256,2048]{3,2,0,1:T(8,128)(2,1)S(1)} %bitcast.190), channel_id=1, replica_groups=mesh['dp'=4,'tp'=8] {'tp'}, dimensions={1} | all-to-all | bytes 16777216 | tf_op jit(solution)/shard_map/all_to_all | solution.py:21
  590.0 1.8 convert_reduce_fusion.1
  591.8 0.3 fusion.115
  592.1 0.4 multiply_reduce_fusion
  592.5 1.4 add_convert_fusion
  593.9 0.1 all-gather.11.cloned.1.call-update
  594.0 46.8 %all-gather.11.cloned.1.call-done = bf16[1,2048,2048]{2,1,0:T(8,128)(2,1)} async-done(((bf16[1,256,2048]{2,1,0:T(8,128)(2,1)}), bf16[1,2048,2048]{2,1,0:T(8,128)(2,1)}) %all-gather.11.cloned.1.call-update) | async-done | bytes 8388624 | tf_op jit(solution)/shard_map/all_gather | solution.py:40
  640.8 25.3 %convolution_convert_fusion = bf16[2048,2048]{1,0:T(8,128)(2,1)} fusion(bf16[1,2048,2048]{2,1,0:T(8,128)(2,1)} %all-gather.11.cloned.1.call-done, bf16[2,1024,2048]{2,1,0:T(8,128)(2,1)} %param.22, f32[1024]{0:T(1024)S(1)} %bitcast.208, bf16[2,2048,1024]{2,1,0:T(8,128)(2,1)} %param.20), kind=kOutput, calls=%fused_computation.51 | convolution fusion | flops 17205035008 | bytes 25169920 | tf_op jit(solution)/shard_map/bsf,fd->bsd/dot_general | solution.py:43
  666.1 97.5 %all_to_all.21 = bf16[1,8,256,2048]{3,2,0,1:T(8,128)(2,1)S(1)} all-to-all(bf16[1,8,256,2048]{3,2,0,1:T(8,128)(2,1)} %bitcast.192), channel_id=1, replica_groups=mesh['dp'=4,'tp'=8] {'tp'}, dimensions={1} | all-to-all | bytes 16777216 | tf_op jit(solution)/shard_map/all_to_all | solution.py:21
  763.6 1.8 convert_reduce_fusion
  765.4 1.3 fusion.93
  (20 shorter events, 0.1 us)
Async XLA Ops:
  6.5 58.6 %all-gather.5.cloned.1.call-start = ((), (), s32[]{:S(2)}) async-start(), calls=%async_computation.4 | async-start | bytes 9437184 | tf_op jit(solution)/shard_map/all_gather | solution.py:32
  94.3 14.4 %copy-start.4 = (bf16[2,2,128,2048]{3,2,1,0:T(8,128)(2,1)S(1)}, bf16[2,2,128,2048]{3,2,1,0:T(8,128)(2,1)}, u32[]{:S(2)}) copy-start(bf16[2,2,128,2048]{3,2,1,0:T(8,128)(2,1)} %param.18) | copy-start | bytes 6291460
  113.3 5.5 copy-start.6
  113.3 5.5 copy-start.7
  113.3 5.5 copy-start.8
  113.3 98.9 %all-to-all-start = ((bf16[1,8,256,2048]{3,2,0,1:T(8,128)(2,1)}), bf16[1,8,256,2048]{3,2,0,1:T(8,128)(2,1)}, u32[]{:S(2)}, u32[]{:S(2)}) async-start(bf16[1,8,256,2048]{3,2,0,1:T(8,128)(2,1)} %bitcast.189), calls=%async_computation | async-start | bytes 16777216 | tf_op jit(solution)/shard_map/all_to_all | solution.py:21
  118.6 148.2 %all-gather.7.cloned.1.call-start = ((), (), s32[]{:S(2)}) async-start(), calls=%async_computation.5 | async-start | bytes 9437184 | tf_op jit(solution)/shard_map/all_gather | solution.py:40
  118.8 98.6 %copy-start = (bf16[1,256,2048]{2,1,0:T(8,128)(2,1)S(1)}, bf16[1,256,2048]{2,1,0:T(8,128)(2,1)}, u32[]{:S(2)}) copy-start(bf16[1,256,2048]{2,1,0:T(8,128)(2,1)} %param.12) | copy-start | bytes 3145732
  217.9 2.1 copy-start.10
  292.0 5.7 copy-start.9
  292.1 98.9 %all-to-all-start.1 = ((bf16[1,8,256,2048]{3,2,0,1:T(8,128)(2,1)}), bf16[1,8,256,2048]{3,2,0,1:T(8,128)(2,1)}, u32[]{:S(2)}, u32[]{:S(2)}) async-start(bf16[1,8,256,2048]{3,2,0,1:T(8,128)(2,1)} %bitcast.191), calls=%async_computation.1 | async-start | bytes 16777216 | tf_op jit(solution)/shard_map/all_to_all | solution.py:21
  297.4 149.3 %all-gather.9.cloned.1.call-start = ((), (), s32[]{:S(2)}) async-start(), calls=%async_computation.6 | async-start | bytes 9437184 | tf_op jit(solution)/shard_map/all_gather | solution.py:32
  397.1 1.4 copy-start.1
  397.1 49.5 %copy-start.3 = (bf16[1,2048,3,2,128]{4,3,2,1,0:T(2,128)(2,1)S(1)}, bf16[1,2048,3,2,128]{4,3,2,1,0:T(2,128)(2,1)}, u32[]{:S(2)}) copy-start(bf16[1,2048,3,2,128]{4,3,2,1,0:T(2,128)(2,1)} %get-tuple-element.9) | copy-start | bytes 9437188
  400.0 240.8 %all-gather.11.cloned.1.call-start = ((), (), s32[]{:S(2)}) async-start(), calls=%async_computation.7 | async-start | bytes 9437184 | tf_op jit(solution)/shard_map/all_gather | solution.py:40
  475.9 14.4 %copy-start.5 = (bf16[2,2,128,2048]{3,2,1,0:T(8,128)(2,1)S(1)}, bf16[2,2,128,2048]{3,2,1,0:T(8,128)(2,1)}, u32[]{:S(2)}) copy-start(bf16[2,2,128,2048]{3,2,1,0:T(8,128)(2,1)} %param.18) | copy-start | bytes 6291460
  590.0 1.8 copy-start.2
Sparse Core Ops, SparseCore 0:
  14.1 50.9 all-gather.4
  220.1 46.5 all-gather.6
  400.1 46.5 all-gather.8
  594.1 46.6 all-gather.10
where the time goes:
time: 777 us; the launch traced here: 773 us
  waiting for transfers between devices  365 us (47%)
  blocking collectives  195 us (25%)
  matrix products  145 us (19%)
  other arithmetic  32.6 us (4%)
  between operations  13.6 us (2%)
  starting transfers between devices  11.2 us (1%)
  local copies, waits for them, and re-layouts  11 us (1%)
    all_to_all x2, blocking collectives, scatter_rows(): received = lax.all_to_all(pieces, 'tp', 1, 1, tiled=True)  195 us
    all_to_all x2, waiting for transfers between devices, scatter_rows(): received = lax.all_to_all(pieces, 'tp', 1, 1, tiled=True)  186 us
    all_gather x2, waiting for transfers between devices, local_forward(): gathered_mlp = lax.all_gather(normed_mlp, 'tp', axis=1, tiled=True)  93.5 us
    all_gather x2, waiting for transfers between devices, local_forward(): gathered = lax.all_gather(normed, 'tp', axis=1, tiled=True)  85.2 us
    dot_general x2, matrix products, local_forward(): jnp.einsum('bsf,fd->bsd', hidden, w_down[layer], preferred_element_type=j...  50.6 us
    sub x2, matrix products, local_forward(): jax.nn.softmax(jnp.where(causal, scores, -1e+30), axis=-1)  38 us
    dot_general x2, matrix products, local_forward(): jnp.einsum('bhqk,bhke->bhqe', attn_probs, qkv_proj[2], preferred_element_...  28.8 us
    dot_general x2, matrix products, local_forward(): jnp.einsum('bsd,dthe->tbhse', gathered, w_qkv[layer], preferred_element_t...  20.4 us
  transfers between devices with their start and end apart: 6, of which 6 were waited for; matrix products, arithmetic and copies ran while one was open for 2% of the time, Pallas kernels for 0%

commit v1 on v0

v1 whole, which is shorter than its diff:
```python
import functools
import math
import jax
import jax.numpy as jnp
from jax import lax
from jax.experimental import pallas as pl
from jax.experimental.pallas import tpu as pltpu
from jax.sharding import PartitionSpec as P

F32 = jnp.float32
BF16 = jnp.bfloat16
MESH = pl.DeviceIdType.MESH
OPP, RIGHT, LEFT, OWN = range(4)


def pick(i, values):
    out = values[0]
    for n in range(1, len(values)):
        out = jnp.where(i == n, values[n], out)
    return out


def decoder(tp_size, layers, heads, head_dim,
            x_ref, g1_ref, s1_ref, g2_ref, s2_ref, bo_ref, bu_ref, bd_ref,
            wqkv_hbm, wout_hbm, wup_hbm, wdown_hbm,
            y_ref,
            hid, qkv, resid, acc, pst, prv, snd, rcv, scores, mask, mlp, att,
            wqkv, wout, wup, wdown,
            wsem, ag_ss, ag_rs, rs_ss, rs_rs):
    chips = tp_size // 2
    rows, width = x_ref.shape
    half, quarter = rows // 2, rows // 4
    hd = heads * head_dim
    scale = 1.0 / math.sqrt(head_dim)
    me = lax.axis_index("tp")
    chip = me // 2
    core = lax.rem(me, 2)
    right = lax.rem(me + 2, tp_size)
    left = lax.rem(me + tp_size - 2, tp_size)
    mate = me + 1 - 2 * core
    chip_of = [lax.rem(chip + 2, chips), lax.rem(chip + 1, chips), lax.rem(chip + chips - 1, chips), chip]
    top, low = pl.ds(0, quarter), pl.ds(quarter, quarter)
    mine, other = pl.ds(0, half), pl.ds(half, half)

    def remote(src, dst, ss, rs, s, k, to):
        return pltpu.make_async_remote_copy(src, dst, ss.at[s, k], rs.at[s, k], device_id={"tp": to}, device_id_type=MESH)

    def gather_copy(s, k):
        if k < 3:
            blk = hid.at[chip if k < 2 else chip_of[LEFT], s, top if k == 1 else low]
            return remote(blk, blk, ag_ss, ag_rs, s, k, right)
        if k < 6:
            blk = hid.at[chip if k < 5 else chip_of[RIGHT], s, low if k == 4 else top]
            return remote(blk, blk, ag_ss, ag_rs, s, k, left)
        c = chip_of[k - 6]
        return remote(hid.at[c, s, mine], hid.at[c, s, other], ag_ss, ag_rs, s, k, mate)

    def gather_send(s):
        for k in (0, 3, 6 + OWN, 1, 4):
            gather_copy(s, k).start()

    def gather_first(s):
        gather_copy(s, 0).wait_recv()
        gather_copy(s, 2).start()
        gather_copy(s, 3).wait_recv()
        gather_copy(s, 5).start()

    def gather_second(s):
        gather_copy(s, 1).wait_recv()
        gather_copy(s, 6 + LEFT).start()
        gather_copy(s, 4).wait_recv()
        gather_copy(s, 6 + RIGHT).start()

    def gather_third(s):
        gather_copy(s, 2).wait_recv()
        gather_copy(s, 5).wait_recv()
        gather_copy(s, 6 + OPP).start()

    def gather_mate(s, kind):
        gather_copy(s, 6 + kind).wait_recv()

    def sum_copy(s, k):
        if k < 6:
            return remote(snd.at[s, k], rcv.at[s, k], rs_ss, rs_rs, s, k, right if k < 3 else left)
        return remote(pst.at[s, k - 6], prv.at[s, k - 6], rs_ss, rs_rs, s, k, mate)

    def mate_send(s, kind):
        remote(pst.at[s, kind], prv.at[s, kind], rs_ss, rs_rs, s, 6 + kind, mate).start()

    step = 16

    def combine(s, kind, r0, dst, extra):
        @pl.loop(0, quarter // step)
        def _(t):
            at = pl.ds(pl.multiple_of(r0 + t * step, step), step)
            at0 = pl.ds(pl.multiple_of(t * step, step), step)
            total = acc[s, kind, at, :] + prv[s, kind, at, :].astype(F32)
            if extra is not None:
                total = total + rcv[s, extra, at0, :].astype(F32)
            snd[s, dst, at0, :] = total.astype(BF16)

    def send_opp(s):
        for k in (2, 5, 6, 7, 8, 9):
            gather_copy(s, k).wait_send()
        sum_copy(s, 6 + OPP).wait_recv()
        combine(s, OPP, quarter, 0, None)
        sum_copy(s, 0).start()
        combine(s, OPP, 0, 3, None)
        sum_copy(s, 3).start()

    def send_near(s):
        sum_copy(s, 6 + RIGHT).wait_recv()
        combine(s, RIGHT, 0, 1, None)
        sum_copy(s, 1).start()
        sum_copy(s, 6 + LEFT).wait_recv()
        combine(s, LEFT, quarter, 4, None)
        sum_copy(s, 4).start()

    def send_through(s):
        sum_copy(s, 0).wait_recv()
        combine(s, RIGHT, quarter, 2, 0)
        sum_copy(s, 2).start()
        sum_copy(s, 3).wait_recv()
        combine(s, LEFT, 0, 5, 3)
        sum_copy(s, 5).start()

    def norm_row(s, at0, r, gain_ref, shift_ref, layer):
        mean = jnp.mean(r, axis=-1, keepdims=True)
        centered = r - mean
        var = jnp.mean(centered * centered, axis=-1, keepdims=True)
        normed = centered * lax.rsqrt(var + 1e-5) * gain_ref[pl.ds(layer, 1), :] + shift_ref[pl.ds(layer, 1), :]
        hid[chip, s, at0, :] = normed.astype(BF16)

    def finish(s, layer, bias_ref, gain_ref, shift_ref, next_layer, last):
        for k in (1, 2, 4, 5, 6 + OWN):
            sum_copy(s, k).wait_recv()
        for k in range(10):
            sum_copy(s, k).wait_send()
        for k in (0, 1, 3, 4):
            gather_copy(s, k).wait_send()
        for part, a, b in ((0, 1, 5), (1, 2, 4)):
            @pl.loop(0, quarter // step)
            def _(t):
                at0 = pl.ds(pl.multiple_of(t * step, step), step)
                at = pl.ds(pl.multiple_of(part * quarter + t * step, step), step)
                rat = pl.ds(pl.multiple_of(s * half + part * quarter + t * step, step), step)
                total = acc[s, OWN, at, :] + prv[s, OWN, at, :].astype(F32)
                total = total + (rcv[s, a, at0, :].astype(F32) + rcv[s, b, at0, :].astype(F32))
                r = resid[rat, :] + (total + bias_ref[pl.ds(layer, 1), :])
                resid[rat, :] = r
                if last is None:
                    norm_row(s, at, r, gain_ref, shift_ref, next_layer)
                else:
                    @pl.when(last)
                    def _():
                        y_ref[rat, :] = r.astype(BF16)

                    @pl.when(jnp.logical_not(last))
                    def _():
                        norm_row(s, at, r, gain_ref, shift_ref, next_layer)
        if last is None:
            gather_send(s)
        else:
            @pl.when(jnp.logical_not(last))
            def _():
                gather_send(s)

    def block_at(s):
        return pl.ds(pl.multiple_of(s * rows, rows), rows)

    def do_qkv(s, d):
        @pl.loop(0, 3)
        def _(n):
            cols = pl.ds(pl.multiple_of(n * hd, hd), hd)
            qkv[d, block_at(s), cols] = jnp.dot(hid[d, s], wqkv[:, cols], preferred_element_type=F32).astype(BF16)

    def project(s, kind, lhs_ref, w_ref):
        tile = min(256, width)

        @pl.loop(0, width // tile)
        def _(n):
            cols = pl.ds(pl.multiple_of(n * tile, tile), tile)
            part = jnp.dot(lhs_ref[...], w_ref[:, cols], preferred_element_type=F32)
            acc[s, kind, :, cols] = part[:half]
            pst[s, kind, :, cols] = part[half:].astype(BF16)
        mate_send(s, kind)

    def do_mlp(s, d, kind, layer):
        hidden = wup.shape[1]
        tile = min(256, hidden)

        @pl.loop(0, hidden // tile)
        def _(n):
            cols = pl.ds(pl.multiple_of(n * tile, tile), tile)
            pre = jnp.dot(hid[d, s], wup[:, cols], preferred_element_type=F32) + bu_ref[pl.ds(layer, 1), cols]
            mlp[:, cols] = jax.nn.gelu(pre, approximate=True).astype(BF16)
        project(s, kind, mlp, wdown)

    def do_attention(s, d, kind):
        lanes = head_dim
        for h in range(heads):
            q = qkv[d, block_at(s), h * head_dim:(h + 1) * head_dim]

            def score(k):
                keys = qkv[k, :, hd + h * head_dim:hd + (h + 1) * head_dim]
                return lax.dot_general(q, keys, (((1,), (1,)), ((), ())), preferred_element_type=F32) * scale

            def fold(op, into, tile):
                for j in range(tile.shape[1] // lanes):
                    into = op(into, tile[:, j * lanes:(j + 1) * lanes])
                return into

            def first(k, top_so_far):
                sc = score(k)
                scores[k] = sc
                return fold(jnp.maximum, top_so_far, sc)

            peak = lax.fori_loop(0, d, first, jnp.full((rows, lanes), -1e30, F32))
            sc = jnp.where(mask[s] > 0.0, score(d), -1e30)
            scores[d] = sc
            peak = jnp.max(fold(jnp.maximum, peak, sc), axis=-1, keepdims=True)

            def second(k, total):
                e = jnp.exp(scores[k] - peak)
                scores[k] = e
                return fold(jnp.add, total, e)

            total = lax.fori_loop(0, d + 1, second, jnp.zeros((rows, lanes), F32))
            inv = 1.0 / jnp.sum(total, axis=-1, keepdims=True)

            def third(k, out):
                p = (scores[k] * inv).astype(BF16)
                vals = qkv[k, :, 2 * hd + h * head_dim:2 * hd + (h + 1) * head_dim]
                return out + jnp.dot(p, vals, preferred_element_type=F32)

            out = lax.fori_loop(0, d + 1, third, jnp.zeros((rows, head_dim), F32))
            att[:, h * head_dim:(h + 1) * head_dim] = out.astype(BF16)
        project(s, kind, att, wout)

    weights = ((wqkv_hbm, wqkv), (wout_hbm, wout), (wup_hbm, wup), (wdown_hbm, wdown))

    def weight_copy(n, layer):
        return pltpu.make_async_copy(weights[n][0].at[layer], weights[n][1], wsem.at[n])

    def next_weights(layer, which):
        @pl.when(layer + 1 < layers)
        def _():
            for n in which:
                weight_copy(n, layer + 1).start()

    for n in range(4):
        weight_copy(n, 0).start()

    barrier = pltpu.get_barrier_semaphore()
    for peer in (left, right, mate):
        pl.semaphore_signal(barrier, inc=1, device_id={"tp": peer}, device_id_type=MESH)
    pl.semaphore_wait(barrier, 3)

    for s in (0, 1):
        @pl.loop(0, half // step)
        def _(t):
            at = pl.ds(pl.multiple_of(t * step, step), step)
            rat = pl.ds(pl.multiple_of(s * half + t * step, step), step)
            r = x_ref[rat, :].astype(F32)
            resid[rat, :] = r
            norm_row(s, at, r, g1_ref, s1_ref, 0)
        gather_send(s)

    key = lax.broadcasted_iota(jnp.int32, (rows, 2 * rows), 1)
    key_core = jnp.where(lax.rem(key, rows) < half, core, 1 - core)
    key_at = key_core * rows + jnp.where(key < rows, 0, half) + lax.rem(key, half)
    qry = lax.broadcasted_iota(jnp.int32, (rows, 2 * rows), 0)
    qry_at = jnp.where(qry < half, core, 1 - core) * rows + lax.rem(qry, half)
    for s in (0, 1):
        mask[s] = (key_at <= qry_at + s * half).astype(F32)

    gather_order = [(OWN, 0), (LEFT, 0), (RIGHT, 0), (OPP, 0), (OWN, 1), (LEFT, 1), (RIGHT, 1), (OPP, 1)]
    sum_order = [(OPP, 0), (OPP, 1), (RIGHT, 0), (LEFT, 0), (OWN, 0), (RIGHT, 1), (LEFT, 1), (OWN, 1)]

    def run(order, before, work, after):
        @pl.loop(0, len(order))
        def _(i):
            for n in range(len(order)):
                if n in before:
                    pl.when(i == n)(before[n])
            kind = pick(i, [k for k, _ in order])
            work(pick(i, [s for _, s in order]), pick(i, [chip_of[k] for k, _ in order]), kind)
            for n in range(len(order)):
                if n in after:
                    pl.when(i == n)(after[n])

    def layer_body(layer, _):
        def arrive(extra):
            def at0():
                gather_mate(0, OWN)

            def at1():
                gather_first(0)
                gather_second(0)
                gather_mate(0, LEFT)
                gather_mate(0, RIGHT)

            def at3():
                gather_first(1)
                gather_third(0)
                gather_mate(0, OPP)

            def at4():
                gather_mate(1, OWN)

            def at5():
                gather_second(1)
                if extra:
                    send_opp(0)
                    send_near(0)
                gather_mate(1, LEFT)
                gather_mate(1, RIGHT)

            def at7():
                gather_third(1)
                gather_mate(1, OPP)
            return {0: at0, 1: at1, 3: at3, 4: at4, 5: at5, 7: at7}

        weight_copy(0, layer).wait()
        run(gather_order, arrive(False), lambda s, d, kind: do_qkv(s, d), {})
        next_weights(layer, (0,))

        weight_copy(1, layer).wait()

        def after3():
            send_near(0)
            send_through(0)

        def after6():
            send_near(1)
            send_through(1)

        run(sum_order, {}, do_attention, {0: lambda: send_opp(0), 1: lambda: send_opp(1), 3: after3, 6: after6})
        next_weights(layer, (1,))
        for s in (0, 1):
            finish(s, layer, bo_ref, g2_ref, s2_ref, layer, None)

        weight_copy(2, layer).wait()
        weight_copy(3, layer).wait()
        run(gather_order, arrive(True), lambda s, d, kind: do_mlp(s, d, kind, layer), {})
        next_weights(layer, (2, 3))
        send_through(0)
        send_opp(1)
        send_near(1)
        send_through(1)
        last = layer == layers - 1
        for s in (0, 1):
            finish(s, layer, bd_ref, g1_ref, s1_ref, jnp.minimum(layer + 1, layers - 1), last)
        return 0

    lax.fori_loop(0, layers, layer_body, 0)


def solution(mesh):
    tp_size = mesh.shape["tp"]

    def local_forward(x_local, ln1_gain, ln1_bias, ln2_gain, ln2_bias, w_qkv, w_out, b_out, w_up, b_up, w_down, b_down):
        batch, rows, width = x_local.shape
        layers, _, _, heads, head_dim = w_qkv.shape
        hidden = w_up.shape[2]
        hd = heads * head_dim
        chips = tp_size // 2
        half, quarter = rows // 2, rows // 4
        vmem = pl.BlockSpec(memory_space=pltpu.VMEM)
        anywhere = pl.BlockSpec(memory_space=pl.ANY)
        call = pl.pallas_call(
            functools.partial(decoder, tp_size, layers, heads, head_dim),
            out_shape=jax.ShapeDtypeStruct((rows, width), BF16),
            in_specs=[vmem] * 8 + [anywhere] * 4,
            out_specs=vmem,
            scratch_shapes=[
                pltpu.VMEM((chips, 2, rows, width), BF16),
                pltpu.VMEM((chips, 2 * rows, 3 * hd), BF16),
                pltpu.VMEM((rows, width), F32),
                pltpu.VMEM((2, 4, half, width), F32),
                pltpu.VMEM((2, 4, half, width), BF16),
                pltpu.VMEM((2, 4, half, width), BF16),
                pltpu.VMEM((2, 6, quarter, width), BF16),
                pltpu.VMEM((2, 6, quarter, width), BF16),
                pltpu.VMEM((chips, rows, 2 * rows), F32),
                pltpu.VMEM((2, rows, 2 * rows), F32),
                pltpu.VMEM((rows, hidden), BF16),
                pltpu.VMEM((rows, hd), BF16),
                pltpu.VMEM((width, 3 * hd), BF16),
                pltpu.VMEM((hd, width), BF16),
                pltpu.VMEM((width, hidden), BF16),
                pltpu.VMEM((hidden, width), BF16),
                pltpu.SemaphoreType.DMA((4,)),
                pltpu.SemaphoreType.DMA((2, 10)),
                pltpu.SemaphoreType.DMA((2, 10)),
                pltpu.SemaphoreType.DMA((2, 10)),
                pltpu.SemaphoreType.DMA((2, 10)),
            ],
            compiler_params=pltpu.CompilerParams(collective_id=0, has_side_effects=True, vmem_limit_bytes=64 * 1024 * 1024 - 128 * 1024),
        )
        y = call(
            x_local.reshape(rows, width), ln1_gain, ln1_bias, ln2_gain, ln2_bias, b_out, b_up, b_down,
            w_qkv.reshape(layers, width, 3 * hd), w_out.reshape(layers, hd, width), w_up, w_down,
        )
        return y.reshape(batch, rows, width)

    rows_spec = P("dp", "tp", None)
    in_specs = (rows_spec, P(), P(), P(), P(), P(None, None, None, "tp", None), P(None, "tp", None, None), P(), P(None, None, "tp"), P(None, "tp"), P(None, "tp", None), P())
    return jax.shard_map(local_forward, mesh=mesh, in_specs=in_specs, out_specs=rows_spec, check_vma=False)
```

time: 777 us -> 388 us (0.50)
  Pallas kernels: 0 us -> 370 us
  waiting for transfers between devices: 365 us -> 0 us
  blocking collectives: 195 us -> 0 us
  matrix products: 145 us -> 0 us
  other arithmetic: 32.6 us -> 0 us
  between operations: 13.6 us -> 0.01 us
  starting transfers between devices: 11.2 us -> 0 us
    pallas_call x0 -> x1, Pallas kernels: none -> 370 us  [local_forward(): call(x_local.reshape(rows, width), ln1_gain, ln1_bias, ln2_gain, ln2_bias...]
    all_to_all x2 -> x0, blocking collectives: 195 us -> none  [scatter_rows(): received = lax.all_to_all(pieces, 'tp', 1, 1, tiled=True)]
    all_to_all x2 -> x0, waiting for transfers between devices: 186 us -> none  [scatter_rows(): received = lax.all_to_all(pieces, 'tp', 1, 1, tiled=True)]
    all_gather x4 -> x0, waiting for transfers between devices: 179 us -> none  [the longest x2 93.5 us: local_forward(): gathered_mlp = lax.all_gather(normed_mlp, 'tp', axis=1, tiled=True)]
    dot_general x8 -> x0, matrix products: 107 us -> none  [the longest x2 50.6 us: local_forward(): jnp.einsum('bsf,fd->bsd', hidden, w_down[layer], preferred_element_type=j...]
    sub x2 -> x0, matrix products: 38 us -> none  [local_forward(): jax.nn.softmax(jnp.where(causal, scores, -1e+30), axis=-1)]
    reduce_sum x12 -> x0, other arithmetic: 20 us -> none  [the longest x4 14.3 us: scatter_rows(): return jnp.sum(received.astype(jnp.float32), axis=1)]
    reshape x0 -> x1, local copies, waits for them, and re-layouts: none -> 14.6 us  [local_forward(): w_qkv.reshape(layers, width, 3 * hd)]
  transfers between devices with their start and end apart: 6 -> 0, of which waited for: 6 -> 0; matrix products, arithmetic and copies ran while one was open for 2% -> 0% of each run, Pallas kernels for 0% -> 0%
where the time goes in v1:
time: 388 us; the launch traced here: 387 us
  Pallas kernels  370 us (95%)
  local copies, waits for them, and re-layouts  16.9 us (4%)
    pallas_call x1, Pallas kernels, local_forward(): call(x_local.reshape(rows, width), ln1_gain, ln1_bias, ln2_gain, ln2_bias...  370 us
    reshape x1, local copies, waits for them, and re-layouts, local_forward(): w_qkv.reshape(layers, width, 3 * hd)  14.6 us

profile of v1, /device:TPU:81, one launch (start us, length us, event | category | flops | bytes accessed | tf_op | source)
XLA Modules:
  0.0 386.9 jit_solution(16534517518277624765)
XLA Ops:
  0.0 14.6 %reshape.13.wqkv_hbm = bf16[2,2048,768]{2,1,0:T(8,128)(2,1)} reshape(bf16[2,2048,3,2,128]{4,3,2,1,0:T(2,128)(2,1)} %param.17) | data formatting | bytes 12582912 | tf_op jit(solution)/shard_map/reshape | solution.py:403
  14.6 370.0 %shard_map.118 = bf16[256,2048]{1,0:T(8,128)(2,1)} custom-call(bf16[256,2048]{1,0:T(8,128)(2,1)} %bitcast.5, f32[2,2048]{1,0:T(2,128)} %g1_ref.1, f32[2,2048]{1,0:T(2,128)} %s1_ref.1, f32[2,2048]{1,0:T(2,128)} %g2_ref.1, f32[2,2048]{1,0:T(2,128)} %s2_ref.1, f32[2,2048]{1,0:T(2,128)} %bo_ref.1, f32[2,1024]{1,0:T(2,128)} %bu_ref.1, f32[2,2048]{1,0:T(2,128)} %bd_ref.1, ...), custom_call_target="tpu_custom_call" | custom-call | tf_op jit(solution)/shard_map/pallas_call | solution.py:401
  384.6 2.3 copy.14

commit v2 on v1

--- a/solution.py
+++ b/solution.py
@@ -24,8 +24,8 @@
             x_ref, g1_ref, s1_ref, g2_ref, s2_ref, bo_ref, bu_ref, bd_ref,
             wqkv_hbm, wout_hbm, wup_hbm, wdown_hbm,
             y_ref,
-            hid, qkv, resid, acc, pst, prv, snd, rcv, scores, mask, mlp, att,
-            wqkv, wout, wup, wdown,
+            hid, qk, vt, resid, acc, pst, prv, snd, rcv, scores, mask, mlp, att,
+            wraw, order_ref, wqkv, wout, wup, wdown,
             wsem, ag_ss, ag_rs, rs_ss, rs_rs):
     chips = tp_size // 2
     rows, width = x_ref.shape
@@ -100,8 +100,7 @@
             snd[s, dst, at0, :] = total.astype(BF16)
 
     def send_opp(s):
-        for k in (2, 5, 6, 7, 8, 9):
-            gather_copy(s, k).wait_send()
+        gather_copy(s, 6 + OPP).wait_send()
         sum_copy(s, 6 + OPP).wait_recv()
         combine(s, OPP, quarter, 0, None)
         sum_copy(s, 0).start()
@@ -117,6 +116,8 @@
         sum_copy(s, 4).start()
 
     def send_through(s):
+        for k in (2, 5, 6 + RIGHT, 6 + LEFT):
+            gather_copy(s, k).wait_send()
         sum_copy(s, 0).wait_recv()
         combine(s, RIGHT, quarter, 2, 0)
         sum_copy(s, 2).start()
@@ -136,7 +137,7 @@
             sum_copy(s, k).wait_recv()
         for k in range(10):
             sum_copy(s, k).wait_send()
-        for k in (0, 1, 3, 4):
+        for k in (0, 1, 3, 4, 6 + OWN):
             gather_copy(s, k).wait_send()
         for part, a, b in ((0, 1, 5), (1, 2, 4)):
             @pl.loop(0, quarter // step)
@@ -169,13 +170,12 @@
         return pl.ds(pl.multiple_of(s * rows, rows), rows)
 
     def do_qkv(s, d):
-        @pl.loop(0, 3)
-        def _(n):
-            cols = pl.ds(pl.multiple_of(n * hd, hd), hd)
-            qkv[d, block_at(s), cols] = jnp.dot(hid[d, s], wqkv[:, cols], preferred_element_type=F32).astype(BF16)
+        out = jnp.dot(hid[d, s], wqkv[...], preferred_element_type=F32)
+        qk[d, block_at(s), :] = out[:, :2 * hd].astype(BF16)
+        vt[d, :, block_at(s)] = jnp.transpose(out[:, 2 * hd:]).astype(BF16)
 
     def project(s, kind, lhs_ref, w_ref):
-        tile = min(256, width)
+        tile = min(1024, width)
 
         @pl.loop(0, width // tile)
         def _(n):
@@ -187,7 +187,7 @@
 
     def do_mlp(s, d, kind, layer):
         hidden = wup.shape[1]
-        tile = min(256, hidden)
+        tile = min(1024, hidden)
 
         @pl.loop(0, hidden // tile)
         def _(n):
@@ -196,48 +196,42 @@
             mlp[:, cols] = jax.nn.gelu(pre, approximate=True).astype(BF16)
         project(s, kind, mlp, wdown)
 
+    def attend(s, d):
+        keys, lanes = 2 * rows, 8
+        for h in range(heads):
+            at = slice(h * head_dim, (h + 1) * head_dim)
+            q = qk[d, block_at(s), at]
+            peak = None
+            for k in range(d + 1):
+                sc = lax.dot_general(qk[k, :, hd + h * head_dim:hd + (h + 1) * head_dim], q, (((1,), (1,)), ((), ())), preferred_element_type=F32)
+                if k == d:
+                    sc = jnp.where(mask[s] > 0.0, sc, -3e38)
+                scores[h, k] = sc
+                top_here = jnp.max(sc.reshape(keys // lanes, lanes, rows), axis=0)
+                peak = top_here if peak is None else jnp.maximum(peak, top_here)
+            peak = jnp.max(peak, axis=0, keepdims=True)
+            total = None
+            for k in range(d + 1):
+                e = jnp.exp2((scores[h, k] - peak) * (scale * math.log2(math.e)))
+                scores[h, k] = e
+                here = jnp.sum(e.reshape(keys // lanes, lanes, rows), axis=0)
+                total = here if total is None else total + here
+            inv = 1.0 / jnp.sum(total, axis=0, keepdims=True)
+            out = None
+            for k in range(d + 1):
+                p = (scores[h, k] * inv).astype(BF16)
+                here = jnp.dot(vt[k, at, :], p, preferred_element_type=F32)
+                out = here if out is None else out + here
+            att[:, at] = jnp.transpose(out).astype(BF16)
+
     def do_attention(s, d, kind):
-        lanes = head_dim
-        for h in range(heads):
-            q = qkv[d, block_at(s), h * head_dim:(h + 1) * head_dim]
-
-            def score(k):
-                keys = qkv[k, :, hd + h * head_dim:hd + (h + 1) * head_dim]
-                return lax.dot_general(q, keys, (((1,), (1,)), ((), ())), preferred_element_type=F32) * scale
-
-            def fold(op, into, tile):
-                for j in range(tile.shape[1] // lanes):
-                    into = op(into, tile[:, j * lanes:(j + 1) * lanes])
-                return into
-
-            def first(k, top_so_far):
-                sc = score(k)
-                scores[k] = sc
-                return fold(jnp.maximum, top_so_far, sc)
-
-            peak = lax.fori_loop(0, d, first, jnp.full((rows, lanes), -1e30, F32))
-            sc = jnp.where(mask[s] > 0.0, score(d), -1e30)
-            scores[d] = sc
-            peak = jnp.max(fold(jnp.maximum, peak, sc), axis=-1, keepdims=True)
-
-            def second(k, total):
-                e = jnp.exp(scores[k] - peak)
-                scores[k] = e
-                return fold(jnp.add, total, e)
-
-            total = lax.fori_loop(0, d + 1, second, jnp.zeros((rows, lanes), F32))
-            inv = 1.0 / jnp.sum(total, axis=-1, keepdims=True)
-
-            def third(k, out):
-                p = (scores[k] * inv).astype(BF16)
-                vals = qkv[k, :, 2 * hd + h * head_dim:2 * hd + (h + 1) * head_dim]
-                return out + jnp.dot(p, vals, preferred_element_type=F32)
-
-            out = lax.fori_loop(0, d + 1, third, jnp.zeros((rows, head_dim), F32))
-            att[:, h * head_dim:(h + 1) * head_dim] = out.astype(BF16)
+        for n in range(chips):
+            @pl.when(d == n)
+            def _():
+                attend(s, n)
         project(s, kind, att, wout)
 
-    weights = ((wqkv_hbm, wqkv), (wout_hbm, wout), (wup_hbm, wup), (wdown_hbm, wdown))
+    weights = ((wqkv_hbm, wraw), (wout_hbm, wout), (wup_hbm, wup), (wdown_hbm, wdown))
 
     def weight_copy(n, layer):
         return pltpu.make_async_copy(weights[n][0].at[layer], weights[n][1], wsem.at[n])
@@ -254,8 +248,6 @@
     barrier = pltpu.get_barrier_semaphore()
     for peer in (left, right, mate):
         pl.semaphore_signal(barrier, inc=1, device_id={"tp": peer}, device_id_type=MESH)
-    pl.semaphore_wait(barrier, 3)
-
     for s in (0, 1):
         @pl.loop(0, half // step)
         def _(t):
@@ -264,17 +256,33 @@
             r = x_ref[rat, :].astype(F32)
             resid[rat, :] = r
             norm_row(s, at, r, g1_ref, s1_ref, 0)
+        if s == 0:
+            pl.semaphore_wait(barrier, 3)
         gather_send(s)
 
-    key = lax.broadcasted_iota(jnp.int32, (rows, 2 * rows), 1)
+    key = lax.broadcasted_iota(jnp.int32, (2 * rows, rows), 0)
     key_core = jnp.where(lax.rem(key, rows) < half, core, 1 - core)
     key_at = key_core * rows + jnp.where(key < rows, 0, half) + lax.rem(key, half)
-    qry = lax.broadcasted_iota(jnp.int32, (rows, 2 * rows), 0)
+    qry = lax.broadcasted_iota(jnp.int32, (2 * rows, rows), 1)
     qry_at = jnp.where(qry < half, core, 1 - core) * rows + lax.rem(qry, half)
     for s in (0, 1):
         mask[s] = (key_at <= qry_at + s * half).astype(F32)
 
-    gather_order = [(OWN, 0), (LEFT, 0), (RIGHT, 0), (OPP, 0), (OWN, 1), (LEFT, 1), (RIGHT, 1), (OPP, 1)]
+    parts = 3 * heads
+    to = lax.broadcasted_iota(jnp.int32, (parts * 128, parts * 128), 0)
+    come = lax.broadcasted_iota(jnp.int32, (parts * 128, parts * 128), 1)
+    order_ref[...] = (come == lax.rem(to, 128) * parts + to // 128).astype(BF16)
+
+    def sort_wqkv():
+        @pl.loop(0, width // 128)
+        def _(n):
+            rows_in = pl.ds(pl.multiple_of(n * parts * 128, 128), parts * 128)
+            rows_out = pl.ds(pl.multiple_of(n * 128, 128), 128)
+            moved = jnp.dot(order_ref[...], wraw[rows_in, :], preferred_element_type=F32).astype(BF16)
+            for p in range(parts):
+                wqkv[rows_out, p * head_dim:(p + 1) * head_dim] = moved[p * 128:(p + 1) * 128]
+
+    gather_order = [(OWN, 0), (LEFT, 0), (RIGHT, 0), (OWN, 1), (LEFT, 1), (RIGHT, 1), (OPP, 0), (OPP, 1)]
     sum_order = [(OPP, 0), (OPP, 1), (RIGHT, 0), (LEFT, 0), (OWN, 0), (RIGHT, 1), (LEFT, 1), (OWN, 1)]
 
     def run(order, before, work, after):
@@ -301,29 +309,33 @@
                 gather_mate(0, RIGHT)
 
             def at3():
+                gather_mate(1, OWN)
+
+            def at4():
                 gather_first(1)
+                gather_second(1)
+                gather_mate(1, LEFT)
+                gather_mate(1, RIGHT)
+
+            def at6():
+                if extra:
+                    send_near(0)
                 gather_third(0)
                 gather_mate(0, OPP)
 
-            def at4():
-                gather_mate(1, OWN)
-
-            def at5():
-                gather_second(1)
+            def at7():
+                if extra:
+                    send_near(1)
+                gather_third(1)
                 if extra:
                     send_opp(0)
-                    send_near(0)
-                gather_mate(1, LEFT)
-                gather_mate(1, RIGHT)
-
-            def at7():
-                gather_third(1)
                 gather_mate(1, OPP)
-            return {0: at0, 1: at1, 3: at3, 4: at4, 5: at5, 7: at7}
+            return {0: at0, 1: at1, 3: at3, 4: at4, 6: at6, 7: at7}
 
         weight_copy(0, layer).wait()
+        sort_wqkv()
+        next_weights(layer, (0,))
         run(gather_order, arrive(False), lambda s, d, kind: do_qkv(s, d), {})
-        next_weights(layer, (0,))
 
         weight_copy(1, layer).wait()
 
@@ -344,9 +356,8 @@
         weight_copy(3, layer).wait()
         run(gather_order, arrive(True), lambda s, d, kind: do_mlp(s, d, kind, layer), {})
         next_weights(layer, (2, 3))
+        send_opp(1)
         send_through(0)
-        send_opp(1)
-        send_near(1)
         send_through(1)
         last = layer == layers - 1
         for s in (0, 1):
@@ -375,17 +386,20 @@
             out_specs=vmem,
             scratch_shapes=[
                 pltpu.VMEM((chips, 2, rows, width), BF16),
-                pltpu.VMEM((chips, 2 * rows, 3 * hd), BF16),
+                pltpu.VMEM((chips, 2 * rows, 2 * hd), BF16),
+                pltpu.VMEM((chips, hd, 2 * rows), BF16),
                 pltpu.VMEM((rows, width), F32),
                 pltpu.VMEM((2, 4, half, width), F32),
                 pltpu.VMEM((2, 4, half, width), BF16),
                 pltpu.VMEM((2, 4, half, width), BF16),
                 pltpu.VMEM((2, 6, quarter, width), BF16),
                 pltpu.VMEM((2, 6, quarter, width), BF16),
-                pltpu.VMEM((chips, rows, 2 * rows), F32),
-                pltpu.VMEM((2, rows, 2 * rows), F32),
+                pltpu.VMEM((heads, chips, 2 * rows, rows), F32),
+                pltpu.VMEM((2, 2 * rows, rows), F32),
                 pltpu.VMEM((rows, hidden), BF16),
                 pltpu.VMEM((rows, hd), BF16),
+                pltpu.VMEM((3 * heads * width, head_dim), BF16),
+                pltpu.VMEM((3 * heads * 128, 3 * heads * 128), BF16),
                 pltpu.VMEM((width, 3 * hd), BF16),
                 pltpu.VMEM((hd, width), BF16),
                 pltpu.VMEM((width, hidden), BF16),
@@ -400,7 +414,7 @@
         )
         y = call(
             x_local.reshape(rows, width), ln1_gain, ln1_bias, ln2_gain, ln2_bias, b_out, b_up, b_down,
-            w_qkv.reshape(layers, width, 3 * hd), w_out.reshape(layers, hd, width), w_up, w_down,
+            w_qkv.reshape(layers, width * 3 * heads, head_dim), w_out.reshape(layers, hd, width), w_up, w_down,
         )
         return y.reshape(batch, rows, width)
 

time: 388 us -> 301 us (0.78)
  Pallas kernels: 370 us -> 298 us
  local copies, waits for them, and re-layouts: 16.9 us -> 2.3 us
    pallas_call x1, Pallas kernels: 370 us -> 298 us  [local_forward(): call(x_local.reshape(rows, width), ln1_gain, ln1_bias, ln2_gain, ln2_bias...]
    reshape x1 -> x0, local copies, waits for them, and re-layouts: 14.6 us -> none  [local_forward(): w_qkv.reshape(layers, width, 3 * hd)]
where the time goes in v2:
time: 301 us
  Pallas kernels  298 us (99%)
    pallas_call x1, Pallas kernels, local_forward(): call(x_local.reshape(rows, width), ln1_gain, ln1_bias, ln2_gain, ln2_bias...  298 us

profile of v2, /device:TPU:81, one launch (start us, length us, event | category | flops | bytes accessed | tf_op | source)
XLA Modules:
  0.0 300.8 jit_solution(6591229710597045763)
XLA Ops:
  0.0 298.4 %shard_map.118 = bf16[256,2048]{1,0:T(8,128)(2,1)} custom-call(bf16[256,2048]{1,0:T(8,128)(2,1)} %bitcast.7, f32[2,2048]{1,0:T(2,128)} %g1_ref.1, f32[2,2048]{1,0:T(2,128)} %s1_ref.1, f32[2,2048]{1,0:T(2,128)} %g2_ref.1, f32[2,2048]{1,0:T(2,128)} %s2_ref.1, f32[2,2048]{1,0:T(2,128)} %bo_ref.1, f32[2,1024]{1,0:T(2,128)} %bu_ref.1, f32[2,2048]{1,0:T(2,128)} %bd_ref.1, ...), custom_call_target="tpu_custom_call" | custom-call | tf_op jit(solution)/shard_map/pallas_call | solution.py:415
  298.5 2.3 copy.14

commit v3 on v2

--- a/solution.py
+++ b/solution.py
@@ -20,13 +20,13 @@
     return out
 
 
-def decoder(tp_size, layers, heads, head_dim,
+def decoder(tp_size, sharers, layers, heads, head_dim,
             x_ref, g1_ref, s1_ref, g2_ref, s2_ref, bo_ref, bu_ref, bd_ref,
             wqkv_hbm, wout_hbm, wup_hbm, wdown_hbm,
-            y_ref,
-            hid, qk, vt, resid, acc, pst, prv, snd, rcv, scores, mask, mlp, att,
+            y_ref, wg,
+            hid, qk, vt, resid, acc, pst, prv, snd, rcv, scores, mask, mlp, att, heads_in,
             wraw, order_ref, wqkv, wout, wup, wdown,
-            wsem, ag_ss, ag_rs, rs_ss, rs_rs):
+            wsem, lsem, ag_ss, ag_rs, rs_ss, rs_rs, hs_ss, hs_rs, wo_ss, wo_rs):
     chips = tp_size // 2
     rows, width = x_ref.shape
     half, quarter = rows // 2, rows // 4
@@ -38,6 +38,9 @@
     right = lax.rem(me + 2, tp_size)
     left = lax.rem(me + tp_size - 2, tp_size)
     mate = me + 1 - 2 * core
+    opposite = lax.rem(me + tp_size // 2, tp_size)
+    group = lax.axis_index("dp")
+    side = lax.rem(group, sharers)
     chip_of = [lax.rem(chip + 2, chips), lax.rem(chip + 1, chips), lax.rem(chip + chips - 1, chips), chip]
     top, low = pl.ds(0, quarter), pl.ds(quarter, quarter)
     mine, other = pl.ds(0, half), pl.ds(half, half)
@@ -55,8 +58,86 @@
         c = chip_of[k - 6]
         return remote(hid.at[c, s, mine], hid.at[c, s, other], ag_ss, ag_rs, s, k, mate)
 
-    def gather_send(s):
-        for k in (0, 3, 6 + OWN, 1, 4):
+    part = hd // sharers
+    piece = part // 2
+    to_mate = 6 + 3 * (sharers - 1)
+    wout_copies = to_mate + 4
+
+    def wout_copy(layer, k):
+        def rows_at(off, size):
+            return pl.ds(pl.multiple_of(side * part + off, piece), size)
+
+        def go(src, dst, to):
+            return pltpu.make_async_remote_copy(src, dst, wo_ss.at[layer, k], wo_rs.at[layer, k], device_id=to, device_id_type=MESH)
+
+        if k < 6:
+            at = rows_at(piece if k in (0, 2, 4) else 0, piece)
+            to = {"tp": right if k < 3 else left}
+            if k in (2, 5):
+                blk = wg.at[layer, left if k == 2 else right, at]
+                return go(blk, blk, to)
+            return go(wout_hbm.at[layer, at], wg.at[layer, me, at], to)
+        if k < to_mate + 3:
+            shard = (left, right, opposite)[k % 3]
+            if k < to_mate:
+                blk = wg.at[layer, shard, rows_at(0, part)]
+                return go(blk, blk, {"dp": group - side + lax.rem(side + (k - 6) // 3 + 1, sharers)})
+            return go(wg.at[layer, shard], wg.at[layer, shard], {"tp": mate})
+        return go(wout_hbm.at[layer], wg.at[layer, me], {"tp": mate})
+
+    def wout_begin(layer):
+        for k in (0, 3, 1, 4, to_mate + 3):
+            wout_copy(layer, k).start()
+
+    def wout_pass(layer):
+        for k, onward in ((0, 2), (3, 5)):
+            wout_copy(layer, k).wait_recv()
+            wout_copy(layer, onward).start()
+
+    def wout_share(layer):
+        for k in (1, 4, 2, 5):
+            wout_copy(layer, k).wait_recv()
+        for k in range(6, to_mate):
+            wout_copy(layer, k).start()
+
+    def wout_collect(layer):
+        for k in range(6, to_mate):
+            wout_copy(layer, k).wait_recv()
+        for k in range(to_mate, to_mate + 3):
+            wout_copy(layer, k).start()
+
+    def wout_end(layer):
+        for k in range(to_mate, wout_copies):
+            wout_copy(layer, k).wait_recv()
+        for k in range(wout_copies):
+            wout_copy(layer, k).wait_send()
+
+    others = [(OPP, 0), (RIGHT, 0), (LEFT, 0), (OPP, 1), (RIGHT, 1), (LEFT, 1), (OWN, 1)]
+    seen_from = {OPP: OPP, RIGHT: LEFT, LEFT: RIGHT, OWN: OWN}
+
+    def device_at(kind, across):
+        return chip_of[kind] * 2 + (1 - core if across else core)
+
+    def wout_load(layer, n):
+        kept = pst.at[pl.ds(n * hd, hd)] if n < 4 else snd.at[pl.ds((n - 4) * hd, hd)]
+        return pltpu.make_async_copy(wg.at[layer, device_at(*others[n])], kept, lsem.at[n])
+
+    def heads_copy(s, kind, across):
+        slot = 1 + others.index((seen_from[kind], across))
+        k = 2 * kind + across
+        return pltpu.make_async_remote_copy(
+            att.at[s, kind, other if across else mine], heads_in.at[s, :, pl.ds(slot * hd, hd)],
+            hs_ss.at[s, k], hs_rs.at[s, k], device_id={"tp": device_at(kind, across)}, device_id_type=MESH)
+
+    def send_heads(s, kind):
+        for across in (0, 1):
+            if (kind, across) == (OWN, 0):
+                heads_in[s, :, :hd] = att[s, OWN, mine, :]
+            else:
+                heads_copy(s, kind, across).start()
+
+    def gather_send(s, which=(0, 3, 6 + OWN, 1, 4)):
+        for k in which:
             gather_copy(s, k).start()
 
     def gather_first(s):
@@ -81,11 +162,14 @@
 
     def sum_copy(s, k):
         if k < 6:
-            return remote(snd.at[s, k], rcv.at[s, k], rs_ss, rs_rs, s, k, right if k < 3 else left)
-        return remote(pst.at[s, k - 6], prv.at[s, k - 6], rs_ss, rs_rs, s, k, mate)
+            return remote(snd.at[pl.ds((s * 6 + k) * quarter, quarter)], rcv.at[s, k], rs_ss, rs_rs, s, k, right if k < 3 else left)
+        return remote(pst.at[pl.ds((s * 4 + k - 6) * half, half)], prv.at[s, k - 6], rs_ss, rs_rs, s, k, mate)
+
+    def staged(s, kind):
+        return pl.ds(pl.multiple_of((s * 4 + kind) * half, half), half)
 
     def mate_send(s, kind):
-        remote(pst.at[s, kind], prv.at[s, kind], rs_ss, rs_rs, s, 6 + kind, mate).start()
+        remote(pst.at[staged(s, kind)], prv.at[s, kind], rs_ss, rs_rs, s, 6 + kind, mate).start()
 
     step = 16
 
@@ -97,7 +181,7 @@
             total = acc[s, kind, at, :] + prv[s, kind, at, :].astype(F32)
             if extra is not None:
                 total = total + rcv[s, extra, at0, :].astype(F32)
-            snd[s, dst, at0, :] = total.astype(BF16)
+            snd[pl.ds(pl.multiple_of((s * 6 + dst) * quarter + t * step, step), step), :] = total.astype(BF16)
 
     def send_opp(s):
         gather_copy(s, 6 + OPP).wait_send()
@@ -139,12 +223,12 @@
             sum_copy(s, k).wait_send()
         for k in (0, 1, 3, 4, 6 + OWN):
             gather_copy(s, k).wait_send()
-        for part, a, b in ((0, 1, 5), (1, 2, 4)):
+        for which, a, b in ((0, 1, 5), (1, 2, 4)):
             @pl.loop(0, quarter // step)
             def _(t):
                 at0 = pl.ds(pl.multiple_of(t * step, step), step)
-                at = pl.ds(pl.multiple_of(part * quarter + t * step, step), step)
-                rat = pl.ds(pl.multiple_of(s * half + part * quarter + t * step, step), step)
+                at = pl.ds(pl.multiple_of(which * quarter + t * step, step), step)
+                rat = pl.ds(pl.multiple_of(s * half + which * quarter + t * step, step), step)
                 total = acc[s, OWN, at, :] + prv[s, OWN, at, :].astype(F32)
                 total = total + (rcv[s, a, at0, :].astype(F32) + rcv[s, b, at0, :].astype(F32))
                 r = resid[rat, :] + (total + bias_ref[pl.ds(layer, 1), :])
@@ -166,6 +250,30 @@
             def _():
                 gather_send(s)
 
+    def finish_attention(s, layer):
+        for kind, across in others:
+            heads_copy(s, kind, across).wait_recv()
+        for kind, across in others:
+            heads_copy(s, kind, across).wait_send()
+        for k in (0, 1, 3, 4, 6 + OWN):
+            gather_copy(s, k).wait_send()
+        tile = min(512, width)
+        mid = 5 * hd
+
+        @pl.loop(0, width // tile)
+        def _(n):
+            cols = pl.ds(pl.multiple_of(n * tile, tile), tile)
+            total = jnp.dot(heads_in[s, :, :hd], wout[:, cols], preferred_element_type=F32)
+            total = total + jnp.dot(heads_in[s, :, hd:mid], pst[:mid - hd, cols], preferred_element_type=F32)
+            total = total + jnp.dot(heads_in[s, :, mid:], snd[:tp_size * hd - mid, cols], preferred_element_type=F32)
+            at = pl.ds(s * half, half)
+            resid[at, cols] = resid[at, cols] + (total + bo_ref[pl.ds(layer, 1), cols])
+
+        @pl.loop(0, half // step)
+        def _(t):
+            at = pl.ds(pl.multiple_of(t * step, step), step)
+            norm_row(s, at, resid[pl.ds(pl.multiple_of(s * half + t * step, step), step), :], g2_ref, s2_ref, layer)
+
     def block_at(s):
         return pl.ds(pl.multiple_of(s * rows, rows), rows)
 
@@ -180,9 +288,9 @@
         @pl.loop(0, width // tile)
         def _(n):
             cols = pl.ds(pl.multiple_of(n * tile, tile), tile)
-            part = jnp.dot(lhs_ref[...], w_ref[:, cols], preferred_element_type=F32)
-            acc[s, kind, :, cols] = part[:half]
-            pst[s, kind, :, cols] = part[half:].astype(BF16)
+            total = jnp.dot(lhs_ref[...], w_ref[:, cols], preferred_element_type=F32)
+            acc[s, kind, :, cols] = total[:half]
+            pst[staged(s, kind), cols] = total[half:].astype(BF16)
         mate_send(s, kind)
 
     def do_mlp(s, d, kind, layer):
@@ -196,7 +304,7 @@
             mlp[:, cols] = jax.nn.gelu(pre, approximate=True).astype(BF16)
         project(s, kind, mlp, wdown)
 
-    def attend(s, d):
+    def attend(s, d, kind):
         keys, lanes = 2 * rows, 8
         for h in range(heads):
             at = slice(h * head_dim, (h + 1) * head_dim)
@@ -222,14 +330,13 @@
                 p = (scores[h, k] * inv).astype(BF16)
                 here = jnp.dot(vt[k, at, :], p, preferred_element_type=F32)
                 out = here if out is None else out + here
-            att[:, at] = jnp.transpose(out).astype(BF16)
+            att[s, kind, :, at] = jnp.transpose(out).astype(BF16)
 
     def do_attention(s, d, kind):
         for n in range(chips):
             @pl.when(d == n)
             def _():
-                attend(s, n)
-        project(s, kind, att, wout)
+                attend(s, n, kind)
 
     weights = ((wqkv_hbm, wraw), (wout_hbm, wout), (wup_hbm, wup), (wdown_hbm, wdown))
 
@@ -246,8 +353,10 @@
         weight_copy(n, 0).start()
 
     barrier = pltpu.get_barrier_semaphore()
-    for peer in (left, right, mate):
-        pl.semaphore_signal(barrier, inc=1, device_id={"tp": peer}, device_id_type=MESH)
+    for n in range(1, tp_size):
+        pl.semaphore_signal(barrier, inc=1, device_id={"tp": lax.rem(me + n, tp_size)}, device_id_type=MESH)
+    for n in range(1, sharers):
+        pl.semaphore_signal(barrier, inc=1, device_id={"dp": group - side + lax.rem(side + n, sharers)}, device_id_type=MESH)
     for s in (0, 1):
         @pl.loop(0, half // step)
         def _(t):
@@ -257,7 +366,7 @@
             resid[rat, :] = r
             norm_row(s, at, r, g1_ref, s1_ref, 0)
         if s == 0:
-            pl.semaphore_wait(barrier, 3)
+            pl.semaphore_wait(barrier, tp_size + sharers - 2)
         gather_send(s)
 
     key = lax.broadcasted_iota(jnp.int32, (2 * rows, rows), 0)
@@ -284,6 +393,7 @@
 
     gather_order = [(OWN, 0), (LEFT, 0), (RIGHT, 0), (OWN, 1), (LEFT, 1), (RIGHT, 1), (OPP, 0), (OPP, 1)]
     sum_order = [(OPP, 0), (OPP, 1), (RIGHT, 0), (LEFT, 0), (OWN, 0), (RIGHT, 1), (LEFT, 1), (OWN, 1)]
+    heads_order = [(OPP, 0), (RIGHT, 0), (LEFT, 0), (OWN, 0), (OPP, 1), (RIGHT, 1), (LEFT, 1), (OWN, 1)]
 
     def run(order, before, work, after):
         @pl.loop(0, len(order))
@@ -298,12 +408,17 @@
                     pl.when(i == n)(after[n])
 
     def layer_body(layer, _):
-        def arrive(extra):
+        more = layer + 1 < layers
+
+        def arrive(mlp_part):
             def at0():
                 gather_mate(0, OWN)
 
             def at1():
-                gather_first(0)
+                if mlp_part:
+                    pl.when(layer == 0)(lambda: gather_first(0))
+                else:
+                    gather_first(0)
                 gather_second(0)
                 gather_mate(0, LEFT)
                 gather_mate(0, RIGHT)
@@ -314,43 +429,98 @@
             def at4():
                 gather_first(1)
                 gather_second(1)
+                if not mlp_part:
+                    pl.when(layer > 0)(lambda: wout_collect(layer))
                 gather_mate(1, LEFT)
                 gather_mate(1, RIGHT)
 
             def at6():
-                if extra:
+                if mlp_part:
                     send_near(0)
                 gather_third(0)
                 gather_mate(0, OPP)
 
             def at7():
-                if extra:
+                if mlp_part:
                     send_near(1)
                 gather_third(1)
-                if extra:
+                if mlp_part:
                     send_opp(0)
+                else:
+                    pl.when(more)(lambda: wout_begin(layer + 1))
                 gather_mate(1, OPP)
             return {0: at0, 1: at1, 3: at3, 4: at4, 6: at6, 7: at7}
+
+        def with_fetch(before, stage):
+            def act():
+                before()
+                pl.when(more)(lambda: stage(layer + 1))
+            return act
 
         weight_copy(0, layer).wait()
         sort_wqkv()
         next_weights(layer, (0,))
         run(gather_order, arrive(False), lambda s, d, kind: do_qkv(s, d), {})
-
         weight_copy(1, layer).wait()
 
-        def after3():
-            send_near(0)
-            send_through(0)
-
-        def after6():
-            send_near(1)
-            send_through(1)
-
-        run(sum_order, {}, do_attention, {0: lambda: send_opp(0), 1: lambda: send_opp(1), 3: after3, 6: after6})
+        @pl.when(layer == 0)
+        def _():
+            def attend_and_project(s, d, kind):
+                do_attention(s, d, kind)
+                project(s, kind, att.at[s, kind], wout)
+
+            def after3():
+                send_near(0)
+                send_through(0)
+
+            def after6():
+                send_near(1)
+                send_through(1)
+
+            run(sum_order, {}, attend_and_project, {
+                0: with_fetch(lambda: send_opp(0), wout_pass), 1: lambda: send_opp(1),
+                3: with_fetch(after3, wout_share), 6: after6})
+            for s in (0, 1):
+                finish(s, layer, bo_ref, g2_ref, s2_ref, layer, None)
+
+        @pl.when(layer > 0)
+        def _():
+            for s in (0, 1):
+                for k in (2, 5, 6 + OPP, 6 + RIGHT, 6 + LEFT):
+                    gather_copy(s, k).wait_send()
+            wout_end(layer)
+            for n in range(len(others)):
+                wout_load(layer, n).start()
+
+            def with_send(n):
+                def act():
+                    kind, s = heads_order[n]
+                    send_heads(s, kind)
+                return act
+
+            def first_rows():
+                for n in range(len(others)):
+                    wout_load(layer, n).wait()
+                finish_attention(0, layer)
+                gather_send(0, (0, 3, 6 + OWN))
+
+            after = {n: with_send(n) for n in range(8)}
+            if layers > 2:
+                after[0] = with_fetch(after[0], wout_pass)
+                after[3] = with_fetch(after[3], wout_share)
+            send4 = after[4]
+
+            def both4():
+                send4()
+                first_rows()
+            after[4] = both4
+            run(heads_order, {}, do_attention, after)
+            gather_send(0, (1, 4))
+            gather_first(0)
+            finish_attention(1, layer)
+            gather_send(1)
+
         next_weights(layer, (1,))
-        for s in (0, 1):
-            finish(s, layer, bo_ref, g2_ref, s2_ref, layer, None)
 
         weight_copy(2, layer).wait()
         weight_copy(3, layer).wait()
@@ -369,6 +539,7 @@
 
 def solution(mesh):
     tp_size = mesh.shape["tp"]
+    sharers = math.gcd(mesh.shape["dp"], 4)
 
     def local_forward(x_local, ln1_gain, ln1_bias, ln2_gain, ln2_bias, w_qkv, w_out, b_out, w_up, b_up, w_down, b_down):
         batch, rows, width = x_local.shape
@@ -380,24 +551,25 @@
         vmem = pl.BlockSpec(memory_space=pltpu.VMEM)
         anywhere = pl.BlockSpec(memory_space=pl.ANY)
         call = pl.pallas_call(
-            functools.partial(decoder, tp_size, layers, heads, head_dim),
-            out_shape=jax.ShapeDtypeStruct((rows, width), BF16),
+            functools.partial(decoder, tp_size, sharers, layers, heads, head_dim),
+            out_shape=(jax.ShapeDtypeStruct((rows, width), BF16), jax.ShapeDtypeStruct((layers, tp_size, hd, width), BF16)),
             in_specs=[vmem] * 8 + [anywhere] * 4,
-            out_specs=vmem,
+            out_specs=(vmem, anywhere),
             scratch_shapes=[
                 pltpu.VMEM((chips, 2, rows, width), BF16),
                 pltpu.VMEM((chips, 2 * rows, 2 * hd), BF16),
                 pltpu.VMEM((chips, hd, 2 * rows), BF16),
                 pltpu.VMEM((rows, width), F32),
                 pltpu.VMEM((2, 4, half, width), F32),
+                pltpu.VMEM((max(8 * half, 4 * hd), width), BF16),
                 pltpu.VMEM((2, 4, half, width), BF16),
-                pltpu.VMEM((2, 4, half, width), BF16),
-                pltpu.VMEM((2, 6, quarter, width), BF16),
+                pltpu.VMEM((max(12 * quarter, 3 * hd), width), BF16),
                 pltpu.VMEM((2, 6, quarter, width), BF16),
                 pltpu.VMEM((heads, chips, 2 * rows, rows), F32),
                 pltpu.VMEM((2, 2 * rows, rows), F32),
                 pltpu.VMEM((rows, hidden), BF16),
-                pltpu.VMEM((rows, hd), BF16),
+                pltpu.VMEM((2, 4, rows, hd), BF16),
+                pltpu.VMEM((2, half, tp_size * hd), BF16),
                 pltpu.VMEM((3 * heads * width, head_dim), BF16),
                 pltpu.VMEM((3 * heads * 128, 3 * heads * 128), BF16),
                 pltpu.VMEM((width, 3 * hd), BF16),
@@ -405,14 +577,19 @@
                 pltpu.VMEM((width, hidden), BF16),
                 pltpu.VMEM((hidden, width), BF16),
                 pltpu.SemaphoreType.DMA((4,)),
+                pltpu.SemaphoreType.DMA((7,)),
                 pltpu.SemaphoreType.DMA((2, 10)),
                 pltpu.SemaphoreType.DMA((2, 10)),
                 pltpu.SemaphoreType.DMA((2, 10)),
                 pltpu.SemaphoreType.DMA((2, 10)),
+                pltpu.SemaphoreType.DMA((2, 8)),
+                pltpu.SemaphoreType.DMA((2, 8)),
+                pltpu.SemaphoreType.DMA((layers, 7 + 3 * sharers)),
+                pltpu.SemaphoreType.DMA((layers, 7 + 3 * sharers)),
             ],
             compiler_params=pltpu.CompilerParams(collective_id=0, has_side_effects=True, vmem_limit_bytes=64 * 1024 * 1024 - 128 * 1024),
         )
-        y = call(
+        y, _ = call(
             x_local.reshape(rows, width), ln1_gain, ln1_bias, ln2_gain, ln2_bias, b_out, b_up, b_down,
             w_qkv.reshape(layers, width * 3 * heads, head_dim), w_out.reshape(layers, hd, width), w_up, w_down,
         )

time: 301 us -> 290 us (0.963)
  Pallas kernels: 298 us -> 287 us
    pallas_call x1, Pallas kernels: 298 us -> 287 us  [local_forward(): call(x_local.reshape(rows, width), ln1_gain, ln1_bias, ln2_gain, ln2_bias...]
where the time goes in v3:
time: 290 us; the launch traced here: 289 us
  Pallas kernels  287 us (99%)
    pallas_call x1, Pallas kernels, local_forward(): call(x_local.reshape(rows, width), ln1_gain, ln1_bias, ln2_gain, ln2_bias...  287 us

profile of v3, /device:TPU:81, one launch (start us, length us, event | category | flops | bytes accessed | tf_op | source)
XLA Modules:
  0.0 289.3 jit_solution(633491358967284905)
XLA Ops:
  0.0 287.0 %shard_map.118 = (bf16[256,2048]{1,0:T(8,128)(2,1)}, bf16[2,8,256,2048]{3,2,1,0:T(8,128)(2,1)}) custom-call(bf16[256,2048]{1,0:T(8,128)(2,1)} %bitcast.6, f32[2,2048]{1,0:T(2,128)} %g1_ref.1, f32[2,2048]{1,0:T(2,128)} %s1_ref.1, f32[2,2048]{1,0:T(2,128)} %g2_ref.1, f32[2,2048]{1,0:T(2,128)} %s2_ref.1, f32[2,2048]{1,0:T(2,128)} %bo_ref.1, f32[2,1024]{1,0:T(2,128)} %bu_ref.1, ...), custom_call_target="tpu_custom_call" | custom-call | tf_op jit(solution)/shard_map/pallas_call | solution.py:592
  287.0 2.3 copy.14

commit v4 on v3

--- a/solution.py
+++ b/solution.py
@@ -21,14 +21,14 @@
 
 
 def decoder(tp_size, sharers, layers, heads, head_dim,
-            x_ref, g1_ref, s1_ref, g2_ref, s2_ref, bo_ref, bu_ref, bd_ref,
+            x_hbm, g1_ref, s1_ref, g2_ref, s2_ref, bo_ref, bu_ref, bd_ref,
             wqkv_hbm, wout_hbm, wup_hbm, wdown_hbm,
-            y_ref, wg,
-            hid, qk, vt, resid, acc, pst, prv, snd, rcv, scores, mask, mlp, att, heads_in,
+            y_hbm, wg,
+            xy, hid, qk, vt, resid, acc, pst, prv, snd, rcv, scores, mask, mlp, att, heads_in,
             wraw, order_ref, wqkv, wout, wup, wdown,
-            wsem, lsem, ag_ss, ag_rs, rs_ss, rs_rs, hs_ss, hs_rs, wo_ss, wo_rs):
+            wsem, lsem, xsem, ysem, ag_ss, ag_rs, rs_ss, rs_rs, hs_ss, hs_rs, wo_ss, wo_rs):
     chips = tp_size // 2
-    rows, width = x_ref.shape
+    rows, width = xy.shape
     half, quarter = rows // 2, rows // 4
     hd = heads * head_dim
     scale = 1.0 / math.sqrt(head_dim)
@@ -45,6 +45,12 @@
     top, low = pl.ds(0, quarter), pl.ds(quarter, quarter)
     mine, other = pl.ds(0, half), pl.ds(half, half)
 
+    def x_copy(s):
+        return pltpu.make_async_copy(x_hbm.at[pl.ds(s * half, half)], xy.at[pl.ds(s * half, half)], xsem.at[s])
+
+    def y_copy(s):
+        return pltpu.make_async_copy(xy.at[pl.ds(s * half, half)], y_hbm.at[pl.ds(s * half, half)], ysem.at[s])
+
     def remote(src, dst, ss, rs, s, k, to):
         return pltpu.make_async_remote_copy(src, dst, ss.at[s, k], rs.at[s, k], device_id={"tp": to}, device_id_type=MESH)
 
@@ -85,8 +91,12 @@
             return go(wg.at[layer, shard], wg.at[layer, shard], {"tp": mate})
         return go(wout_hbm.at[layer], wg.at[layer, me], {"tp": mate})
 
-    def wout_begin(layer):
-        for k in (0, 3, 1, 4, to_mate + 3):
+    def wout_first(layer):
+        for k in (0, 3):
+            wout_copy(layer, k).start()
+
+    def wout_second(layer):
+        for k in (1, 4):
             wout_copy(layer, k).start()
 
     def wout_pass(layer):
@@ -99,6 +109,7 @@
             wout_copy(layer, k).wait_recv()
         for k in range(6, to_mate):
             wout_copy(layer, k).start()
+        wout_copy(layer, to_mate + 3).start()
 
     def wout_collect(layer):
         for k in range(6, to_mate):
@@ -112,7 +123,7 @@
         for k in range(wout_copies):
             wout_copy(layer, k).wait_send()
 
-    others = [(OPP, 0), (RIGHT, 0), (LEFT, 0), (OPP, 1), (RIGHT, 1), (LEFT, 1), (OWN, 1)]
+    others = [(OPP, 0), (OPP, 1), (LEFT, 0), (LEFT, 1), (RIGHT, 0), (RIGHT, 1), (OWN, 1)]
     seen_from = {OPP: OPP, RIGHT: LEFT, LEFT: RIGHT, OWN: OWN}
 
     def device_at(kind, across):
@@ -174,7 +185,7 @@
     step = 16
 
     def combine(s, kind, r0, dst, extra):
-        @pl.loop(0, quarter // step)
+        @pl.loop(0, quarter // step, unroll=True)
         def _(t):
             at = pl.ds(pl.multiple_of(r0 + t * step, step), step)
             at0 = pl.ds(pl.multiple_of(t * step, step), step)
@@ -224,7 +235,7 @@
         for k in (0, 1, 3, 4, 6 + OWN):
             gather_copy(s, k).wait_send()
         for which, a, b in ((0, 1, 5), (1, 2, 4)):
-            @pl.loop(0, quarter // step)
+            @pl.loop(0, quarter // step, unroll=True)
             def _(t):
                 at0 = pl.ds(pl.multiple_of(t * step, step), step)
                 at = pl.ds(pl.multiple_of(which * quarter + t * step, step), step)
@@ -238,7 +249,7 @@
                 else:
                     @pl.when(last)
                     def _():
-                        y_ref[rat, :] = r.astype(BF16)
+                        xy[rat, :] = r.astype(BF16)
 
                     @pl.when(jnp.logical_not(last))
                     def _():
@@ -246,6 +257,10 @@
         if last is None:
             gather_send(s)
         else:
+            @pl.when(last)
+            def _():
+                y_copy(s).start()
+
             @pl.when(jnp.logical_not(last))
             def _():
                 gather_send(s)
@@ -269,7 +284,7 @@
             at = pl.ds(s * half, half)
             resid[at, cols] = resid[at, cols] + (total + bo_ref[pl.ds(layer, 1), cols])
 
-        @pl.loop(0, half // step)
+        @pl.loop(0, half // step, unroll=4)
         def _(t):
             at = pl.ds(pl.multiple_of(t * step, step), step)
             norm_row(s, at, resid[pl.ds(pl.multiple_of(s * half + t * step, step), step), :], g2_ref, s2_ref, layer)
@@ -349,20 +364,23 @@
             for n in which:
                 weight_copy(n, layer + 1).start()
 
-    for n in range(4):
-        weight_copy(n, 0).start()
-
     barrier = pltpu.get_barrier_semaphore()
     for n in range(1, tp_size):
         pl.semaphore_signal(barrier, inc=1, device_id={"tp": lax.rem(me + n, tp_size)}, device_id_type=MESH)
     for n in range(1, sharers):
         pl.semaphore_signal(barrier, inc=1, device_id={"dp": group - side + lax.rem(side + n, sharers)}, device_id_type=MESH)
     for s in (0, 1):
-        @pl.loop(0, half // step)
+        x_copy(s).start()
+    for n in range(4):
+        weight_copy(n, 0).start()
+    for s in (0, 1):
+        x_copy(s).wait()
+
+        @pl.loop(0, half // step, unroll=4)
         def _(t):
             at = pl.ds(pl.multiple_of(t * step, step), step)
             rat = pl.ds(pl.multiple_of(s * half + t * step, step), step)
-            r = x_ref[rat, :].astype(F32)
+            r = xy[rat, :].astype(F32)
             resid[rat, :] = r
             norm_row(s, at, r, g1_ref, s1_ref, 0)
         if s == 0:
@@ -447,14 +465,17 @@
                 if mlp_part:
                     send_opp(0)
                 else:
-                    pl.when(more)(lambda: wout_begin(layer + 1))
+                    @pl.when(more)
+                    def _():
+                        wout_first(layer + 1)
+                        wout_second(layer + 1)
                 gather_mate(1, OPP)
             return {0: at0, 1: at1, 3: at3, 4: at4, 6: at6, 7: at7}
 
-        def with_fetch(before, stage):
+        def with_fetch(step_work, stage):
             def act():
-                before()
                 pl.when(more)(lambda: stage(layer + 1))
+                step_work()
             return act
 
         weight_copy(0, layer).wait()
@@ -506,8 +527,8 @@
 
             after = {n: with_send(n) for n in range(8)}
             if layers > 2:
-                after[0] = with_fetch(after[0], wout_pass)
-                after[3] = with_fetch(after[3], wout_share)
+                after[1] = with_fetch(after[1], wout_pass)
+                after[5] = with_fetch(after[5], wout_share)
             send4 = after[4]
 
             def both4():
@@ -535,6 +556,8 @@
         return 0
 
     lax.fori_loop(0, layers, layer_body, 0)
+    for s in (0, 1):
+        y_copy(s).wait()
 
 
 def solution(mesh):
@@ -553,9 +576,10 @@
         call = pl.pallas_call(
             functools.partial(decoder, tp_size, sharers, layers, heads, head_dim),
             out_shape=(jax.ShapeDtypeStruct((rows, width), BF16), jax.ShapeDtypeStruct((layers, tp_size, hd, width), BF16)),
-            in_specs=[vmem] * 8 + [anywhere] * 4,
-            out_specs=(vmem, anywhere),
+            in_specs=[anywhere] + [vmem] * 7 + [anywhere] * 4,
+            out_specs=(anywhere, anywhere),
             scratch_shapes=[
+                pltpu.VMEM((rows, width), BF16),
                 pltpu.VMEM((chips, 2, rows, width), BF16),
                 pltpu.VMEM((chips, 2 * rows, 2 * hd), BF16),
                 pltpu.VMEM((chips, hd, 2 * rows), BF16),
@@ -578,6 +602,8 @@
                 pltpu.VMEM((hidden, width), BF16),
                 pltpu.SemaphoreType.DMA((4,)),
                 pltpu.SemaphoreType.DMA((7,)),
+                pltpu.SemaphoreType.DMA((2,)),
+                pltpu.SemaphoreType.DMA((2,)),
                 pltpu.SemaphoreType.DMA((2, 10)),
                 pltpu.SemaphoreType.DMA((2, 10)),
                 pltpu.SemaphoreType.DMA((2, 10)),

time: 290 us -> 287 us (0.990)
  Pallas kernels: 287 us -> 284 us
    pallas_call x1, Pallas kernels: 287 us -> 284 us  [local_forward(): call(x_local.reshape(rows, width), ln1_gain, ln1_bias, ln2_gain, ln2_bias...]
where the time goes in v4:
time: 287 us; the launch traced here: 286 us
  Pallas kernels  284 us (99%)
    pallas_call x1, Pallas kernels, local_forward(): call(x_local.reshape(rows, width), ln1_gain, ln1_bias, ln2_gain, ln2_bias...  284 us

profile of v4, /device:TPU:81, one launch (start us, length us, event | category | flops | bytes accessed | tf_op | source)
XLA Modules:
  0.0 286.4 jit_solution(8059683435828902302)
XLA Ops:
  0.0 284.1 %shard_map.118 = (bf16[256,2048]{1,0:T(8,128)(2,1)}, bf16[2,8,256,2048]{3,2,1,0:T(8,128)(2,1)}) custom-call(bf16[256,2048]{1,0:T(8,128)(2,1)} %bitcast.6, f32[2,2048]{1,0:T(2,128)} %g1_ref.1, f32[2,2048]{1,0:T(2,128)} %s1_ref.1, f32[2,2048]{1,0:T(2,128)} %g2_ref.1, f32[2,2048]{1,0:T(2,128)} %s2_ref.1, f32[2,2048]{1,0:T(2,128)} %bo_ref.1, f32[2,1024]{1,0:T(2,128)} %bu_ref.1, ...), custom_call_target="tpu_custom_call" | custom-call | tf_op jit(solution)/shard_map/pallas_call | solution.py:618
  284.1 2.3 copy.14

commit v5 on v4

--- a/solution.py
+++ b/solution.py
@@ -234,36 +234,37 @@
             sum_copy(s, k).wait_send()
         for k in (0, 1, 3, 4, 6 + OWN):
             gather_copy(s, k).wait_send()
-        for which, a, b in ((0, 1, 5), (1, 2, 4)):
-            @pl.loop(0, quarter // step, unroll=True)
-            def _(t):
-                at0 = pl.ds(pl.multiple_of(t * step, step), step)
-                at = pl.ds(pl.multiple_of(which * quarter + t * step, step), step)
-                rat = pl.ds(pl.multiple_of(s * half + which * quarter + t * step, step), step)
-                total = acc[s, OWN, at, :] + prv[s, OWN, at, :].astype(F32)
-                total = total + (rcv[s, a, at0, :].astype(F32) + rcv[s, b, at0, :].astype(F32))
-                r = resid[rat, :] + (total + bias_ref[pl.ds(layer, 1), :])
-                resid[rat, :] = r
-                if last is None:
-                    norm_row(s, at, r, gain_ref, shift_ref, next_layer)
-                else:
-                    @pl.when(last)
-                    def _():
-                        xy[rat, :] = r.astype(BF16)
-
-                    @pl.when(jnp.logical_not(last))
-                    def _():
-                        norm_row(s, at, r, gain_ref, shift_ref, next_layer)
+        def new_rows(use):
+            for which, a, b in ((0, 1, 5), (1, 2, 4)):
+                @pl.loop(0, quarter // step, unroll=True)
+                def _(t):
+                    at0 = pl.ds(pl.multiple_of(t * step, step), step)
+                    at = pl.ds(pl.multiple_of(which * quarter + t * step, step), step)
+                    rat = pl.ds(pl.multiple_of(s * half + which * quarter + t * step, step), step)
+                    total = acc[s, OWN, at, :] + prv[s, OWN, at, :].astype(F32)
+                    total = total + (rcv[s, a, at0, :].astype(F32) + rcv[s, b, at0, :].astype(F32))
+                    use(at, rat, resid[rat, :] + (total + bias_ref[pl.ds(layer, 1), :]))
+
+        def keep_and_norm(at, rat, r):
+            resid[rat, :] = r
+            norm_row(s, at, r, gain_ref, shift_ref, next_layer)
+
+        def go_on():
+            new_rows(keep_and_norm)
+            gather_send(s)
+
+        def write(at, rat, r):
+            xy[rat, :] = r.astype(BF16)
+
         if last is None:
-            gather_send(s)
+            go_on()
         else:
             @pl.when(last)
             def _():
+                new_rows(write)
                 y_copy(s).start()
 
-            @pl.when(jnp.logical_not(last))
-            def _():
-                gather_send(s)
+            pl.when(jnp.logical_not(last))(go_on)
 
     def finish_attention(s, layer):
         for kind, across in others:
@@ -446,6 +447,8 @@
 
             def at4():
                 gather_first(1)
+                if mlp_part:
+                    send_near(0)
                 gather_second(1)
                 if not mlp_part:
                     pl.when(layer > 0)(lambda: wout_collect(layer))
@@ -453,14 +456,12 @@
                 gather_mate(1, RIGHT)
 
             def at6():
-                if mlp_part:
-                    send_near(0)
                 gather_third(0)
-                gather_mate(0, OPP)
-
-            def at7():
                 if mlp_part:
                     send_near(1)
+                gather_mate(0, OPP)
+
+            def at7():
                 gather_third(1)
                 if mlp_part:
                     send_opp(0)

time: 287 us -> 283 us (0.986)
  Pallas kernels: 284 us -> 280 us
    pallas_call x1, Pallas kernels: 284 us -> 280 us  [local_forward(): call(x_local.reshape(rows, width), ln1_gain, ln1_bias, ln2_gain, ln2_bias...]
where the time goes in v5:
time: 283 us; the launch traced here: 282 us
  Pallas kernels  280 us (99%)
    pallas_call x1, Pallas kernels, local_forward(): call(x_local.reshape(rows, width), ln1_gain, ln1_bias, ln2_gain, ln2_bias...  280 us

profile of v5, /device:TPU:81, one launch (start us, length us, event | category | flops | bytes accessed | tf_op | source)
XLA Modules:
  0.0 282.5 jit_solution(14603036340157565719)
XLA Ops:
  0.0 280.2 %shard_map.118 = (bf16[256,2048]{1,0:T(8,128)(2,1)}, bf16[2,8,256,2048]{3,2,1,0:T(8,128)(2,1)}) custom-call(bf16[256,2048]{1,0:T(8,128)(2,1)} %bitcast.6, f32[2,2048]{1,0:T(2,128)} %g1_ref.1, f32[2,2048]{1,0:T(2,128)} %s1_ref.1, f32[2,2048]{1,0:T(2,128)} %g2_ref.1, f32[2,2048]{1,0:T(2,128)} %s2_ref.1, f32[2,2048]{1,0:T(2,128)} %bo_ref.1, f32[2,1024]{1,0:T(2,128)} %bu_ref.1, ...), custom_call_target="tpu_custom_call" | custom-call | tf_op jit(solution)/shard_map/pallas_call | solution.py:619
  280.2 2.3 copy.14

commit v6 on v5

--- a/solution.py
+++ b/solution.py
@@ -459,17 +459,17 @@
                 gather_third(0)
                 if mlp_part:
                     send_near(1)
-                gather_mate(0, OPP)
-
-            def at7():
-                gather_third(1)
-                if mlp_part:
-                    send_opp(0)
                 else:
                     @pl.when(more)
                     def _():
                         wout_first(layer + 1)
                         wout_second(layer + 1)
+                gather_mate(0, OPP)
+
+            def at7():
+                gather_third(1)
+                if mlp_part:
+                    send_opp(0)
                 gather_mate(1, OPP)
             return {0: at0, 1: at1, 3: at3, 4: at4, 6: at6, 7: at7}
 

time: 283 us -> 282 us (level)
  no operation moved by 1% of the time
where the time goes in v6:
time: 282 us
  Pallas kernels  279 us (99%)
    pallas_call x1, Pallas kernels, local_forward(): call(x_local.reshape(rows, width), ln1_gain, ln1_bias, ln2_gain, ln2_bias...  279 us

profile of v6, /device:TPU:81, one launch (start us, length us, event | category | flops | bytes accessed | tf_op | source)
XLA Modules:
  0.0 281.8 jit_solution(10772875766036058443)
XLA Ops:
  0.0 279.5 %shard_map.118 = (bf16[256,2048]{1,0:T(8,128)(2,1)}, bf16[2,8,256,2048]{3,2,1,0:T(8,128)(2,1)}) custom-call(bf16[256,2048]{1,0:T(8,128)(2,1)} %bitcast.6, f32[2,2048]{1,0:T(2,128)} %g1_ref.1, f32[2,2048]{1,0:T(2,128)} %s1_ref.1, f32[2,2048]{1,0:T(2,128)} %g2_ref.1, f32[2,2048]{1,0:T(2,128)} %s2_ref.1, f32[2,2048]{1,0:T(2,128)} %bo_ref.1, f32[2,1024]{1,0:T(2,128)} %bu_ref.1, ...), custom_call_target="tpu_custom_call" | custom-call | tf_op jit(solution)/shard_map/pallas_call | solution.py:619
  279.5 2.3 copy.14
